TPU v7x, 32 devices: a whole 2x2x4 slice. The times are simulated.
32 devices in a mesh: dp: 8 (over y, x, core), branch: 4 (over z).
Axes of the slice: x: 2, y: 2, z: 4, core: 2. Of those that a mesh axis runs over, the one named last changes fastest.
Arguments:
- image_hidden: bfloat16 [4096, 1024], P('dp', 'branch'), may hold values from -8 to 8
- text_hidden: bfloat16 [4096, 768], P('dp', 'branch'), may hold values from -8 to 8
- image_proj: bfloat16 [1024, 768], replicated, may hold values from -0.1875 to 0.1875
- text_proj: bfloat16 [768, 768], replicated, may hold values from -0.21650635 to 0.21650635
- log_inverse_sharpness: float32 [1], replicated, may hold values from 4 to 5.9
- partner: int32 [4096], replicated, may hold values from 0 to 4095, each once
Outputs:
- loss: float32 [1], replicated
- grad_log_scale: float32 [1], replicated
- grad_image_hidden: bfloat16 [4096, 1024], P('dp', 'branch')
- grad_text_hidden: bfloat16 [4096, 768], P('dp', 'branch')
- grad_image_proj: float32 [1024, 768], P('branch')
- grad_text_proj: float32 [768, 768], P('branch')
Inputs may be any that keep to these rules, and one draw needn't show every extreme that they name: `partner`: each text index appears exactly once.
All inputs are finite; a program needn't handle non-finite values.
Results may differ from a plain program's by a relative error of at most 0.0029.
The roundings to bfloat16 on the way count: a program that leaves them out, or rounds other values in their place, can miss the bound.
Values may be sent and summed in bfloat16 or wider, within the bound.
A program may use at most 64 MiB of HBM per device.

v0:
```python
import jax
import jax.numpy as jnp
from jax import lax
from jax.sharding import PartitionSpec as P

NORM_EPSILON = 1e-06


def normalize(raw_rows):
    lengths = jnp.sqrt(jnp.sum(raw_rows * raw_rows, axis=1, keepdims=True) + NORM_EPSILON)
    unit_rows = raw_rows / lengths
    return (unit_rows, lengths, unit_rows.astype(jnp.bfloat16))


def unnormalize(upstream, unit_rows, lengths):
    radial = jnp.sum(upstream * unit_rows, axis=1, keepdims=True)
    return ((upstream - unit_rows * radial) / lengths).astype(jnp.bfloat16)


def per_device(image_hidden, text_hidden, image_proj, text_proj, log_inverse_sharpness, partner):
    branch_count = lax.axis_size("branch")
    data_count = lax.axis_size("dp")
    branch_pos = lax.axis_index("branch")
    data_pos = lax.axis_index("dp")
    group_rows = image_hidden.shape[0]
    own_rows = group_rows // branch_count
    image_cols = image_hidden.shape[1]
    text_cols = text_hidden.shape[1]
    image_slab = lax.dynamic_slice_in_dim(image_proj, branch_pos * image_cols, image_cols, 0)
    text_slab = lax.dynamic_slice_in_dim(text_proj, branch_pos * text_cols, text_cols, 0)
    image_local, text_local = (
        lax.all_to_all(image_hidden, "branch", split_axis=0, concat_axis=1, tiled=True),
        lax.all_to_all(text_hidden, "branch", split_axis=0, concat_axis=1, tiled=True),
    )
    image_raw = jnp.dot(image_local, image_proj, preferred_element_type=jnp.float32)
    text_raw = jnp.dot(text_local, text_proj, preferred_element_type=jnp.float32)
    image_unit, image_length, image_emb = normalize(image_raw)
    text_unit, text_length, caption_feature_entries = normalize(text_raw)
    normalized_exponent_divisor = jnp.exp(log_inverse_sharpness[0])
    column_count = own_rows * data_count
    total_pairs = group_rows * data_count
    denominator = 2.0 * total_pairs
    group_emb = lax.all_gather(image_emb, "branch", axis=0, tiled=True)
    row_partner = lax.dynamic_slice_in_dim(partner, data_pos * group_rows, group_rows, 0)

    def column_ident(positions):
        return (positions // own_rows * branch_count + branch_pos) * own_rows + positions % own_rows

    block_piece = lax.all_gather(caption_feature_entries, "dp", axis=0, tiled=True)
    row_peak = jnp.full((group_rows,), -jnp.inf, jnp.float32)
    row_mass = jnp.zeros((group_rows,), jnp.float32)
    piece_width = block_piece.shape[0]
    matching_cosine_scores = normalized_exponent_divisor * lax.dot_general(
        group_emb, block_piece, (((1,), (1,)), ((), ())), preferred_element_type=jnp.float32
    )
    logits_kept = matching_cosine_scores
    column_ids = column_ident(jnp.arange(piece_width, dtype=jnp.int32))
    matched = row_partner[:, None] == column_ids[None, :]
    positive = jnp.sum(jnp.where(matched, matching_cosine_scores, 0.0), axis=1)
    new_peak = jnp.max(matching_cosine_scores, axis=1)
    row_mass = row_mass * jnp.exp(row_peak - new_peak) + jnp.sum(
        jnp.exp(matching_cosine_scores - new_peak[:, None]), axis=1
    )
    piece_peak = jnp.max(matching_cosine_scores, axis=0)
    piece_mass = jnp.sum(jnp.exp(matching_cosine_scores - piece_peak[None, :]), axis=0)
    column_peak = piece_peak
    column_mass = piece_mass
    (
        retained_text_rows,
        matching_cosine_scores,
        row_peak,
        row_mass,
        positive,
        column_peak,
        column_mass,
    ) = (block_piece, logits_kept, new_peak, row_mass, positive, column_peak, column_mass)
    row_highest = lax.pmax(row_peak, "branch")
    row_mass, positive = lax.psum((row_mass * jnp.exp(row_peak - row_highest), positive), "branch")
    row_peak = row_highest
    column_highest = lax.pmax(column_peak, "dp")
    column_mass = lax.psum(column_mass * jnp.exp(column_peak - column_highest), "dp")
    column_peak = column_highest
    row_lse = row_peak + jnp.log(row_mass)
    col_lse = column_peak + jnp.log(column_mass)
    column_ids = column_ident(jnp.arange(column_count, dtype=jnp.int32))
    matched = (row_partner[:, None] == column_ids[None, :]).astype(jnp.float32)
    weights = (
        jnp.exp(matching_cosine_scores - row_lse[:, None])
        + jnp.exp(matching_cosine_scores - col_lse[None, :])
        - 2.0 * matched
    ) / denominator
    scale_part = jnp.sum(weights * matching_cosine_scores)
    reduced_width_parameters = weights.astype(jnp.bfloat16)
    picture_projection_matrix = lax.psum_scatter(
        normalized_exponent_divisor
        * jnp.dot(reduced_width_parameters, retained_text_rows, preferred_element_type=jnp.float32),
        "branch",
        scatter_dimension=0,
        tiled=True,
    )
    text_up = lax.psum_scatter(
        normalized_exponent_divisor
        * lax.dot_general(
            reduced_width_parameters,
            group_emb,
            (((0,), (0,)), ((), ())),
            preferred_element_type=jnp.float32,
        ),
        "dp",
        scatter_dimension=0,
        tiled=True,
    )
    image_down = unnormalize(picture_projection_matrix, image_unit, image_length)
    text_down = unnormalize(text_up, text_unit, text_length)
    image_gathered, text_gathered = (
        lax.all_gather(image_down, "branch", axis=0, tiled=True),
        lax.all_gather(text_down, "branch", axis=0, tiled=True),
    )
    grad_image_hidden = jnp.dot(
        image_gathered, image_slab.T, preferred_element_type=jnp.float32
    ).astype(jnp.bfloat16)
    grad_text_hidden = jnp.dot(
        text_gathered, text_slab.T, preferred_element_type=jnp.float32
    ).astype(jnp.bfloat16)
    image_weight = lax.dot_general(
        image_hidden, image_gathered, (((0,), (0,)), ((), ())), preferred_element_type=jnp.float32
    )
    text_weight = lax.dot_general(
        text_hidden, text_gathered, (((0,), (0,)), ((), ())), preferred_element_type=jnp.float32
    )
    grad_image_proj, grad_text_proj = lax.psum((image_weight, text_weight), "dp")
    own_row_terms = lax.dynamic_slice_in_dim(
        row_lse - 2.0 * positive, branch_pos * own_rows, own_rows, 0
    )
    own_col_terms = lax.dynamic_slice_in_dim(col_lse, data_pos * own_rows, own_rows, 0)
    loss_part = (jnp.sum(own_row_terms) + jnp.sum(own_col_terms)) / denominator
    loss_total, scale_total = lax.psum((loss_part, scale_part), ("dp", "branch"))
    return (
        loss_total.reshape(1),
        scale_total.reshape(1),
        grad_image_hidden,
        grad_text_hidden,
        grad_image_proj,
        grad_text_proj,
    )


def solution(mesh):
    placed = (P("dp", "branch"), P("dp", "branch"), P(), P(), P(), P())
    return jax.shard_map(
        per_device,
        mesh=mesh,
        in_specs=placed,
        out_specs=(
            P(),
            P(),
            P("dp", "branch"),
            P("dp", "branch"),
            P("branch", None),
            P("branch", None),
        ),
        check_vma=False,
    )
```

profile of v0, /device:TPU:0, one launch (start us, length us, event | category | flops | bytes accessed | tf_op | source)
XLA Modules:
  0.0 283.1 jit_solution(11487178637805667783)
XLA Ops:
  8.3 13.6 %all_to_all.38 = bf16[4,128,192]{1,2,0:T(8,128)(2,1)S(1)} all-to-all(bf16[4,128,192]{1,2,0:T(8,128)(2,1)S(1)} %copy_bitcast_fusion), channel_id=1, replica_groups=mesh['dp'=8,'branch'=4] {'branch'}, dimensions={0} | all-to-all | bytes 393216 | tf_op jit(solution)/shard_map/all_to_all | solution.py:33
  24.5 3.4 %all-to-all-start = ((bf16[4,128,256]{2,1,0:T(8,128)(2,1)}), bf16[4,128,256]{2,1,0:T(8,128)(2,1)S(1)}, u32[]{:S(2)}, u32[]{:S(2)}) async-start(bf16[4,128,256]{2,1,0:T(8,128)(2,1)} %bitcast.1), calls=%async_computation | async-start | bytes 524288 | tf_op jit(solution)/shard_map/all_to_all | solution.py:32
  29.4 6.6 %all-to-all-done = bf16[4,128,256]{2,1,0:T(8,128)(2,1)S(1)} async-done(((bf16[4,128,256]{2,1,0:T(8,128)(2,1)}), bf16[4,128,256]{2,1,0:T(8,128)(2,1)S(1)}, u32[]{:S(2)}, u32[]{:S(2)}) %all-to-all-start) | async-done | bytes 262176 | tf_op jit(solution)/shard_map/all_to_all | solution.py:32
  36.8 17.6 %all_gather.12 = bf16[512,768]{1,0:T(8,128)(2,1)S(1)} all-gather(bf16[128,768]{1,0:T(8,128)(2,1)S(1)} %fusion.19), channel_id=1, replica_groups=mesh['dp'=8,'branch'=4] {'branch'}, dimensions={0}, use_global_device_ids=true | all-gather | bytes 983040 | tf_op jit(solution)/shard_map/all_gather | solution.py:43
  54.4 3.8 %fusion.23 = (f32[1024]{0:T(1024)S(1)}, f32[512]{0:T(512)S(1)}, f32[512,1024]{1,0:T(8,128)}) fusion(bf16[512,768]{1,0:T(8,128)(2,1)S(1)} %all_gather.12, bf16[1024,768]{1,0:T(8,128)(2,1)} %all-gather.2.cloned.1.call-done, f32[]{:T(128)} %bitcast), kind=kOutput, calls=%fused_computation.55 | convolution fusion | flops 806877696 | bytes 4462596 | tf_op jit(solution)/shard_map/dot_general | solution.py:53
  58.2 10.3 %pmax.14 = f32[512]{0:T(512)S(1)} all-reduce(f32[512]{0:T(512)S(1)} %get-tuple-element.35), channel_id=1, replica_groups=mesh['dp'=8,'branch'=4] {'branch'}, use_global_device_ids=true, to_apply=%region_3.4 | all-reduce | flops 512 | bytes 4096 | tf_op jit(solution)/shard_map/pmax | solution.py:77
  68.5 11.8 %pmax.15 = f32[1024]{0:T(1024)S(1)} all-reduce(f32[1024]{0:T(1024)S(1)} %get-tuple-element.34), channel_id=1, replica_groups=mesh['dp'=8,'branch'=4] {'dp'}, use_global_device_ids=true, to_apply=%region_10.11 | all-reduce | flops 1024 | bytes 8192 | tf_op jit(solution)/shard_map/pmax | solution.py:80
  80.3 2.3 exponential_reduce_fusion
  82.7 11.9 %psum.51 = f32[1024]{0:T(1024)S(1)} all-reduce(f32[1024]{0:T(1024)S(1)} %exponential_multiply_fusion), channel_id=1, replica_groups=mesh['dp'=8,'branch'=4] {'dp'}, use_global_device_ids=true, to_apply=%region_12.13 | all-reduce | flops 1024 | bytes 8192 | tf_op jit(solution)/shard_map/psum | solution.py:81
  94.6 8.4 %psum.49 = f32[512]{0:T(512)S(1)} all-reduce(f32[512]{0:T(512)S(1)} %exponential_multiply_fusion.1), channel_id=1, replica_groups=mesh['dp'=8,'branch'=4] {'branch'}, use_global_device_ids=true, to_apply=%region_5.6 | all-reduce | flops 512 | bytes 4096 | tf_op jit(solution)/shard_map/psum | solution.py:78
  103.0 4.8 %convolution_multiply_fusion.2 = f32[512,768]{1,0:T(8,128)} fusion(bf16[1024,768]{1,0:T(8,128)(2,1)} %all-gather.2.cloned.1.call-done, f32[]{:T(128)} %bitcast, f32[512,1024]{1,0:T(8,128)} %get-tuple-element.44, f32[1024]{0:T(1024)S(1)} %log_add_fusion, f32[512]{0:T(512)S(1)} %log_add_fusion.1, s32[1024]{0:T(1024)S(1)} %fusion.15, s32[512]{0:T(512)S(1)} %dynamic_slice.15), kind=kOutput, calls=%fused_computation.11 | convolution fusion | flops 809893888 | bytes 5255172 | tf_op jit(solution)/shard_map/dot_general | solution.py:96
  107.9 4.8 %convolution_multiply_fusion = f32[1024,768]{1,0:T(8,128)} fusion(bf16[512,768]{1,0:T(8,128)(2,1)S(1)} %all_gather.12, f32[]{:T(128)} %bitcast, f32[512,1024]{1,0:T(8,128)} %get-tuple-element.44, f32[1024]{0:T(1024)S(1)} %log_add_fusion, f32[512]{0:T(512)S(1)} %log_add_fusion.1, s32[1024]{0:T(1024)S(1)} %fusion.15, s32[512]{0:T(512)S(1)} %dynamic_slice.15), kind=kOutput, calls=%fused_computation.9 | convolution fusion | flops 810287104 | bytes 6041604 | tf_op jit(solution)/shard_map/dot_general | solution.py:103
  113.5 3.6 %multiply_reduce_fusion = (f32[]{:T(128)}, f32[512]{0:T(512)S(1)}) fusion(f32[512,1024]{1,0:T(8,128)} %get-tuple-element.44, f32[1024]{0:T(1024)S(1)} %log_add_fusion, f32[512]{0:T(512)S(1)} %log_add_fusion.1, s32[1024]{0:T(1024)S(1)} %fusion.15, s32[512]{0:T(512)S(1)} %dynamic_slice.15), kind=kLoop, calls=%fused_computation.5 | loop fusion | flops 5766655 | bytes 2111492 | tf_op jit(solution)/shard_map/reduce_sum | solution.py:92
  117.1 11.2 %psum.50 = f32[512]{0:T(512)S(1)} all-reduce(f32[512]{0:T(512)S(1)} %get-tuple-element.31), channel_id=1, replica_groups=mesh['dp'=8,'branch'=4] {'branch'}, use_global_device_ids=true, to_apply=%region_7.8 | all-reduce | flops 512 | bytes 4096 | tf_op jit(solution)/shard_map/psum | solution.py:78
  128.3 14.0 %reduce-scatter.3.cloned.1.call-done = f32[128,768]{1,0:T(8,128)} async-done(((f32[512,768]{1,0:T(8,128)}), f32[128,768]{1,0:T(8,128)}) %reduce-scatter.3.cloned.1.call-update) | async-done | bytes 393232 | tf_op jit(solution)/shard_map/reduce_scatter | solution.py:94
  144.6 17.9 %all_gather.14 = bf16[512,768]{1,0:T(8,128)(2,1)S(1)} all-gather(bf16[128,768]{1,0:T(8,128)(2,1)S(1)} %divide_convert_fusion.1), channel_id=1, replica_groups=mesh['dp'=8,'branch'=4] {'branch'}, dimensions={0}, use_global_device_ids=true | all-gather | bytes 983040 | tf_op jit(solution)/shard_map/all_gather | solution.py:116
  162.5 2.2 convolution_bitcast_fusion
  164.8 25.9 %reduce-scatter.5.cloned.1.call-done = f32[128,768]{1,0:T(8,128)} async-done(((f32[1024,768]{1,0:T(8,128)}), f32[128,768]{1,0:T(8,128)}) %reduce-scatter.5.cloned.1.call-update) | async-done | bytes 393232 | tf_op jit(solution)/shard_map/reduce_scatter | solution.py:101
  193.0 19.6 %all_gather.15 = bf16[512,768]{1,0:T(8,128)(2,1)S(1)} all-gather(bf16[128,768]{1,0:T(8,128)(2,1)S(1)} %divide_convert_fusion), channel_id=1, replica_groups=mesh['dp'=8,'branch'=4] {'branch'}, dimensions={0}, use_global_device_ids=true | all-gather | bytes 983040 | tf_op jit(solution)/shard_map/all_gather | solution.py:117
  212.5 2.1 convolution_bitcast_fusion.1
  216.6 38.5 %all-reduce = (f32[1]{0:T(128)}, f32[1]{0:T(128)}) all-reduce(f32[1]{0:T(128)} %bitcast.6, f32[1]{0:T(128)} %bitcast.7), channel_id=1, replica_groups=mesh['dp'=8,'branch'=4] {'dp','branch'}, use_global_device_ids=true, to_apply=%region_14.15 | all-reduce | flops 2 | bytes 16 | tf_op jit(solution)/shard_map/psum | solution.py:137
  256.2 2.0 convolution_convert_fusion.1
  258.3 14.1 %all-reduce.4.cloned.1.call-done = (f32[256,768]{0,1:T(8,128)}, f32[192,768]{1,0:T(8,128)}) async-done(((f32[256,768]{0,1:T(8,128)}, f32[192,768]{1,0:T(8,128)}), (f32[256,768]{0,1:T(8,128)}, f32[192,768]{1,0:T(8,128)})) %all-reduce.4.cloned.1.call-update) | async-done | bytes 1376272 | tf_op jit(solution)/shard_map/psum | solution.py:131
  272.3 2.3 copy.19
  (34 shorter events, 14.4 us)
Async XLA Ops:
  7.2 29.0 %copy-start = (bf16[1024,768]{1,0:T(8,128)(2,1)S(1)}, bf16[1024,768]{1,0:T(8,128)(2,1)}, u32[]{:S(2)}) copy-start(bf16[1024,768]{1,0:T(8,128)(2,1)} %param.8) | copy-start | bytes 4718596
  7.2 47.2 %all-gather.2.cloned.1.call-start = ((), (), s32[]{:S(2)}) async-start(), calls=%async_computation.4 | async-start | bytes 1769472 | tf_op jit(solution)/shard_map/all_gather | solution.py:49
  24.5 11.6 %all-to-all-start = ((bf16[4,128,256]{2,1,0:T(8,128)(2,1)}), bf16[4,128,256]{2,1,0:T(8,128)(2,1)S(1)}, u32[]{:S(2)}, u32[]{:S(2)}) async-start(bf16[4,128,256]{2,1,0:T(8,128)(2,1)} %bitcast.1), calls=%async_computation | async-start | bytes 524288 | tf_op jit(solution)/shard_map/all_to_all | solution.py:32
  27.9 114.4 %reduce-scatter.3.cloned.1.call-start = ((), (), s32[]{:S(2)}) async-start(), calls=%async_computation.5 | async-start | bytes 1966080 | tf_op jit(solution)/shard_map/reduce_scatter | solution.py:94
  107.8 82.8 %reduce-scatter.5.cloned.1.call-start = ((), (), s32[]{:S(2)}) async-start(), calls=%async_computation.6 | async-start | bytes 3538944 | tf_op jit(solution)/shard_map/reduce_scatter | solution.py:101
  112.8 159.6 %all-reduce.4.cloned.1.call-start = ((), (), s32[]{:S(2)}) async-start(), calls=%async_computation.7 | async-start | bytes 2752512 | tf_op jit(solution)/shard_map/psum | solution.py:131
Sparse Core Ops, SparseCore 0:
  24.6 24.6 all-gather.1
  108.0 34.2 reduce-scatter.2
  145.7 44.9 reduce-scatter.4
  214.8 57.5 all-reduce.3
where the time goes:
time: 284 us; the launch traced here: 283 us
  blocking collectives  161 us (57%)
  waiting for transfers between devices  60.6 us (21%)
  matrix products  23.1 us (8%)
  between operations  15.9 us (6%)
  other arithmetic  12.9 us (5%)
  local copies, waits for them, and re-layouts  6.21 us (2%)
  starting transfers between devices  3.58 us (1%)
    psum x1, blocking collectives, per_device(): lax.psum((loss_part, scale_part), ('dp', 'branch'))  38.5 us
    reduce_scatter x1, waiting for transfers between devices, per_device(): lax.psum_scatter(normalized_exponent_divisor * lax.dot_general(reduced_wi...  25.9 us
    all_gather x1, blocking collectives, per_device(): lax.all_gather(text_down, 'branch', axis=0, tiled=True)  19.6 us
    psum x2, blocking collectives, per_device(): lax.psum((row_mass * jnp.exp(row_peak - row_highest), positive), 'branch')  19.6 us
    all_gather x1, blocking collectives, per_device(): lax.all_gather(image_down, 'branch', axis=0, tiled=True)  17.9 us
    all_gather x1, blocking collectives, per_device(): group_emb = lax.all_gather(image_emb, 'branch', axis=0, tiled=True)  17.6 us
    psum x1, waiting for transfers between devices, per_device(): lax.psum((image_weight, text_weight), 'dp')  14.1 us
    reduce_scatter x1, waiting for transfers between devices, per_device(): lax.psum_scatter(normalized_exponent_divisor * jnp.dot(reduced_width_para...  14 us
  transfers between devices with their start and end apart: 5, of which 4 were waited for; matrix products, arithmetic and copies ran while one was open for 7% of the time, Pallas kernels for 0%

commit v1 on v0

--- a/solution.py
+++ b/solution.py
@@ -4,6 +4,20 @@
 from jax.sharding import PartitionSpec as P
 
 NORM_EPSILON = 1e-06
+
+
+def follow_seats_all(field, a_name, out_dim):
+    p_count = lax.axis_size(a_name)
+    base_arr = field
+    inbox = [base_arr]
+    field_out = list(map(lambda i: (i - 1, i), range(1, p_count))) + [(p_count - 1, 0)]
+    for _ in tuple(range(p_count - 1)):
+        base_arr = lax.ppermute(base_arr, a_name, field_out)
+        inbox += [base_arr]
+    finding = jnp.concatenate([*reversed(inbox)], axis=out_dim)
+    return jnp.roll(
+        finding, shift=(lax.axis_index(a_name) + 1) * base_arr.shape[out_dim], axis=out_dim
+    )
 
 
 def normalize(raw_rows):
@@ -40,7 +54,7 @@
     column_count = own_rows * data_count
     total_pairs = group_rows * data_count
     denominator = 2.0 * total_pairs
-    group_emb = lax.all_gather(image_emb, "branch", axis=0, tiled=True)
+    group_emb = follow_seats_all(image_emb, "branch", 0)
     row_partner = lax.dynamic_slice_in_dim(partner, data_pos * group_rows, group_rows, 0)
 
     def column_ident(positions):

time: 284 us -> 291 us (1.025)
  waiting for transfers between devices: 60.6 us -> 83 us
  blocking collectives: 161 us -> 141 us
  local copies, waits for them, and re-layouts: 6.21 us -> 10.4 us
    ppermute x0 -> x3, waiting for transfers between devices: none -> 22.1 us  [follow_seats_all(): base_arr = lax.ppermute(base_arr, a_name, field_out)]
    all_gather x1 -> x0, blocking collectives: 17.6 us -> none  [per_device(): group_emb = lax.all_gather(image_emb, 'branch', axis=0, tiled=True)]
    unnamed x4 -> x14, local copies, waits for them, and re-layouts: 4.21 us -> 8.34 us
  transfers between devices with their start and end apart: 5 -> 8, of which waited for: 4 -> 7; matrix products, arithmetic and copies ran while one was open for 7% -> 9% of each run, Pallas kernels for 0% -> 0%
where the time goes in v1:
time: 291 us; the launch traced here: 290 us
  blocking collectives  141 us (48%)
  waiting for transfers between devices  83 us (29%)
  matrix products  21.6 us (7%)
  between operations  15.9 us (5%)
  other arithmetic  14.5 us (5%)
  local copies, waits for them, and re-layouts  10.4 us (4%)
  starting transfers between devices  3.81 us (1%)
    psum x1, blocking collectives, per_device(): lax.psum((loss_part, scale_part), ('dp', 'branch'))  38.5 us
    reduce_scatter x1, waiting for transfers between devices, per_device(): lax.psum_scatter(normalized_exponent_divisor * lax.dot_general(reduced_wi...  26.8 us
    ppermute x3, waiting for transfers between devices, follow_seats_all(): base_arr = lax.ppermute(base_arr, a_name, field_out)  22.1 us
    all_gather x1, blocking collectives, per_device(): lax.all_gather(text_down, 'branch', axis=0, tiled=True)  19.6 us
    psum x2, blocking collectives, per_device(): lax.psum((row_mass * jnp.exp(row_peak - row_highest), positive), 'branch')  19.5 us
    all_gather x1, blocking collectives, per_device(): lax.all_gather(image_down, 'branch', axis=0, tiled=True)  17.9 us
    reduce_scatter x1, waiting for transfers between devices, per_device(): lax.psum_scatter(normalized_exponent_divisor * jnp.dot(reduced_width_para...  14.5 us
    psum x1, waiting for transfers between devices, per_device(): lax.psum((image_weight, text_weight), 'dp')  14 us
  transfers between devices with their start and end apart: 8, of which 7 were waited for; matrix products, arithmetic and copies ran while one was open for 9% of the time, Pallas kernels for 0%

profile of v1, /device:TPU:0, one launch (start us, length us, event | category | flops | bytes accessed | tf_op | source)
XLA Modules:
  0.0 290.2 jit_solution(16731163911076620700)
XLA Ops:
  8.3 13.6 %all_to_all.38 = bf16[4,128,192]{1,2,0:T(8,128)(2,1)S(1)} all-to-all(bf16[4,128,192]{1,2,0:T(8,128)(2,1)S(1)} %copy_bitcast_fusion), channel_id=1, replica_groups=mesh['dp'=8,'branch'=4] {'branch'}, dimensions={0} | all-to-all | bytes 393216 | tf_op jit(solution)/shard_map/all_to_all | solution.py:47
  21.9 3.4 %all-to-all-start = ((bf16[4,128,256]{2,1,0:T(8,128)(2,1)}), bf16[4,128,256]{2,1,0:T(8,128)(2,1)S(1)}, u32[]{:S(2)}, u32[]{:S(2)}) async-start(bf16[4,128,256]{2,1,0:T(8,128)(2,1)} %bitcast.30), calls=%async_computation | async-start | bytes 524288 | tf_op jit(solution)/shard_map/all_to_all | solution.py:46
  27.9 5.5 %all-to-all-done = bf16[4,128,256]{2,1,0:T(8,128)(2,1)S(1)} async-done(((bf16[4,128,256]{2,1,0:T(8,128)(2,1)}), bf16[4,128,256]{2,1,0:T(8,128)(2,1)S(1)}, u32[]{:S(2)}, u32[]{:S(2)}) %all-to-all-start) | async-done | bytes 262176 | tf_op jit(solution)/shard_map/all_to_all | solution.py:46
  34.5 7.4 %collective-permute-done = bf16[128,768]{1,0:T(8,128)(2,1)S(1)} collective-permute-done((bf16[128,768]{1,0:T(8,128)(2,1)S(1)}, bf16[128,768]{1,0:T(8,128)(2,1)S(1)}, u32[]{:S(2)}, u32[]{:S(2)}) %collective-permute-start) | collective-permute-done | bytes 196640 | tf_op jit(solution)/shard_map/ppermute | solution.py:15
  41.9 8.7 %collective-permute-done.1 = bf16[128,768]{1,0:T(8,128)(2,1)S(1)} collective-permute-done((bf16[128,768]{1,0:T(8,128)(2,1)S(1)}, bf16[128,768]{1,0:T(8,128)(2,1)S(1)}, u32[]{:S(2)}, u32[]{:S(2)}) %collective-permute-start.1) | collective-permute-done | bytes 196640 | tf_op jit(solution)/shard_map/ppermute | solution.py:15
  52.1 6.0 %collective-permute-done.2 = bf16[128,768]{1,0:T(8,128)(2,1)S(1)} collective-permute-done((bf16[128,768]{1,0:T(8,128)(2,1)S(1)}, bf16[128,768]{1,0:T(8,128)(2,1)S(1)}, u32[]{:S(2)}, u32[]{:S(2)}) %collective-permute-start.2) | collective-permute-done | bytes 196640 | tf_op jit(solution)/shard_map/ppermute | solution.py:15
  63.8 4.0 %fusion.27 = (f32[1024]{0:T(1024)S(1)}, f32[512]{0:T(512)S(1)}, f32[512,1024]{1,0:T(8,128)}) fusion(bf16[1024,768]{1,0:T(8,128)(2,1)} %all-gather.2.cloned.1.call-done, bf16[1024,768]{1,0:T(8,128)(2,1)} %constant_dynamic-update-slice_fusion, s32[]{:T(128)S(6)} %select_n.55, f32[]{:T(128)} %bitcast), kind=kOutput, calls=%fused_computation.67 | convolution fusion | flops 806877696 | bytes 4463108 | tf_op jit(solution)/shard_map/dot_general | solution.py:67
  67.8 8.3 %pmax.14 = f32[512]{0:T(512)S(1)} all-reduce(f32[512]{0:T(512)S(1)} %get-tuple-element.35), channel_id=1, replica_groups=mesh['dp'=8,'branch'=4] {'branch'}, use_global_device_ids=true, to_apply=%region_3.4 | all-reduce | flops 512 | bytes 4096 | tf_op jit(solution)/shard_map/pmax | solution.py:91
  76.2 11.8 %pmax.15 = f32[1024]{0:T(1024)S(1)} all-reduce(f32[1024]{0:T(1024)S(1)} %get-tuple-element.34), channel_id=1, replica_groups=mesh['dp'=8,'branch'=4] {'dp'}, use_global_device_ids=true, to_apply=%region_10.11 | all-reduce | flops 1024 | bytes 8192 | tf_op jit(solution)/shard_map/pmax | solution.py:94
  88.0 2.3 exponential_reduce_fusion
  90.3 11.9 %psum.51 = f32[1024]{0:T(1024)S(1)} all-reduce(f32[1024]{0:T(1024)S(1)} %exponential_multiply_fusion), channel_id=1, replica_groups=mesh['dp'=8,'branch'=4] {'dp'}, use_global_device_ids=true, to_apply=%region_12.13 | all-reduce | flops 1024 | bytes 8192 | tf_op jit(solution)/shard_map/psum | solution.py:95
  102.2 10.4 %psum.49 = f32[512]{0:T(512)S(1)} all-reduce(f32[512]{0:T(512)S(1)} %exponential_multiply_fusion.1), channel_id=1, replica_groups=mesh['dp'=8,'branch'=4] {'branch'}, use_global_device_ids=true, to_apply=%region_5.6 | all-reduce | flops 512 | bytes 4096 | tf_op jit(solution)/shard_map/psum | solution.py:92
  112.6 4.8 %convolution_multiply_fusion.2 = f32[512,768]{1,0:T(8,128)} fusion(bf16[1024,768]{1,0:T(8,128)(2,1)} %all-gather.2.cloned.1.call-done, f32[]{:T(128)} %bitcast, f32[512,1024]{1,0:T(8,128)} %get-tuple-element.44, f32[1024]{0:T(1024)S(1)} %log_add_fusion, f32[512]{0:T(512)S(1)} %log_add_fusion.1, s32[1024]{0:T(1024)S(1)} %fusion.17, s32[512]{0:T(512)S(1)} %dynamic_slice.20), kind=kOutput, calls=%fused_computation.11 | convolution fusion | flops 809893888 | bytes 5255172 | tf_op jit(solution)/shard_map/dot_general | solution.py:110
  117.5 5.0 %convolution_multiply_fusion = f32[1024,768]{1,0:T(8,128)} fusion(f32[]{:T(128)} %bitcast, bf16[1024,768]{1,0:T(8,128)(2,1)} %constant_dynamic-update-slice_fusion, s32[]{:T(128)S(6)} %select_n.55, f32[512,1024]{1,0:T(8,128)} %get-tuple-element.44, f32[1024]{0:T(1024)S(1)} %log_add_fusion, f32[512]{0:T(512)S(1)} %log_add_fusion.1, s32[1024]{0:T(1024)S(1)} %fusion.17, ...), kind=kOutput, calls=%fused_computation.9 | convolution fusion | flops 810287104 | bytes 6042116 | tf_op jit(solution)/shard_map/dot_general | solution.py:117
  123.2 3.7 %multiply_reduce_fusion = (f32[]{:T(128)}, f32[512]{0:T(512)S(1)}) fusion(f32[512,1024]{1,0:T(8,128)} %get-tuple-element.44, f32[1024]{0:T(1024)S(1)} %log_add_fusion, f32[512]{0:T(512)S(1)} %log_add_fusion.1, s32[1024]{0:T(1024)S(1)} %fusion.17, s32[512]{0:T(512)S(1)} %dynamic_slice.20), kind=kLoop, calls=%fused_computation.5 | loop fusion | flops 5766655 | bytes 2111492 | tf_op jit(solution)/shard_map/reduce_sum | solution.py:106
  126.9 9.1 %psum.50 = f32[512]{0:T(512)S(1)} all-reduce(f32[512]{0:T(512)S(1)} %get-tuple-element.31), channel_id=1, replica_groups=mesh['dp'=8,'branch'=4] {'branch'}, use_global_device_ids=true, to_apply=%region_7.8 | all-reduce | flops 512 | bytes 4096 | tf_op jit(solution)/shard_map/psum | solution.py:92
  136.0 14.5 %reduce-scatter.3.cloned.1.call-done = f32[128,768]{1,0:T(8,128)} async-done(((f32[512,768]{1,0:T(8,128)}), f32[128,768]{1,0:T(8,128)}) %reduce-scatter.3.cloned.1.call-update) | async-done | bytes 393232 | tf_op jit(solution)/shard_map/reduce_scatter | solution.py:108
  152.8 17.9 %all_gather.10 = bf16[512,768]{1,0:T(8,128)(2,1)S(1)} all-gather(bf16[128,768]{1,0:T(8,128)(2,1)S(1)} %divide_convert_fusion.1), channel_id=1, replica_groups=mesh['dp'=8,'branch'=4] {'branch'}, dimensions={0}, use_global_device_ids=true | all-gather | bytes 983040 | tf_op jit(solution)/shard_map/all_gather | solution.py:130
  172.0 26.8 %reduce-scatter.5.cloned.1.call-done = f32[128,768]{1,0:T(8,128)} async-done(((f32[1024,768]{1,0:T(8,128)}), f32[128,768]{1,0:T(8,128)}) %reduce-scatter.5.cloned.1.call-update) | async-done | bytes 393232 | tf_op jit(solution)/shard_map/reduce_scatter | solution.py:115
  201.1 19.6 %all_gather.11 = bf16[512,768]{1,0:T(8,128)(2,1)S(1)} all-gather(bf16[128,768]{1,0:T(8,128)(2,1)S(1)} %divide_convert_fusion), channel_id=1, replica_groups=mesh['dp'=8,'branch'=4] {'branch'}, dimensions={0}, use_global_device_ids=true | all-gather | bytes 983040 | tf_op jit(solution)/shard_map/all_gather | solution.py:131
  223.8 38.5 %all-reduce = (f32[1]{0:T(128)}, f32[1]{0:T(128)}) all-reduce(f32[1]{0:T(128)} %bitcast.6, f32[1]{0:T(128)} %bitcast.7), channel_id=1, replica_groups=mesh['dp'=8,'branch'=4] {'dp','branch'}, use_global_device_ids=true, to_apply=%region_14.15 | all-reduce | flops 2 | bytes 16 | tf_op jit(solution)/shard_map/psum | solution.py:151
  263.4 2.0 convolution_convert_fusion.1
  265.5 14.0 %all-reduce.4.cloned.1.call-done = (f32[256,768]{0,1:T(8,128)}, f32[192,768]{1,0:T(8,128)}) async-done(((f32[256,768]{0,1:T(8,128)}, f32[192,768]{1,0:T(8,128)}), (f32[256,768]{0,1:T(8,128)}, f32[192,768]{1,0:T(8,128)})) %all-reduce.4.cloned.1.call-update) | async-done | bytes 1376272 | tf_op jit(solution)/shard_map/psum | solution.py:145
  279.5 2.3 copy.19
  (51 shorter events, 22.8 us)
Async XLA Ops:
  7.2 26.4 %copy-start = (bf16[1024,768]{1,0:T(8,128)(2,1)S(1)}, bf16[1024,768]{1,0:T(8,128)(2,1)}, u32[]{:S(2)}) copy-start(bf16[1024,768]{1,0:T(8,128)(2,1)} %param.8) | copy-start | bytes 4718596
  21.9 11.5 %all-to-all-start = ((bf16[4,128,256]{2,1,0:T(8,128)(2,1)}), bf16[4,128,256]{2,1,0:T(8,128)(2,1)S(1)}, u32[]{:S(2)}, u32[]{:S(2)}) async-start(bf16[4,128,256]{2,1,0:T(8,128)(2,1)} %bitcast.30), calls=%async_computation | async-start | bytes 524288 | tf_op jit(solution)/shard_map/all_to_all | solution.py:46
  25.3 38.5 %all-gather.2.cloned.1.call-start = ((), (), s32[]{:S(2)}) async-start(), calls=%async_computation.4 | async-start | bytes 1769472 | tf_op jit(solution)/shard_map/all_gather | solution.py:63
  27.9 122.6 %reduce-scatter.3.cloned.1.call-start = ((), (), s32[]{:S(2)}) async-start(), calls=%async_computation.5 | async-start | bytes 1966080 | tf_op jit(solution)/shard_map/reduce_scatter | solution.py:108
  34.2 7.6 %collective-permute-start = (bf16[128,768]{1,0:T(8,128)(2,1)S(1)}, bf16[128,768]{1,0:T(8,128)(2,1)S(1)}, u32[]{:S(2)}, u32[]{:S(2)}) collective-permute-start(bf16[128,768]{1,0:T(8,128)(2,1)S(1)} %fusion.23), channel_id=1, source_target_pairs={{0,1},{1,2},{2,3},{3,0},{4,5},{5,6},{6,7},{7,4},{8,9},{9,10},{10,1... | collective-permute-start | bytes 589832 | tf_op jit(solution)/shard_map/ppermute | solution.py:15
  41.9 8.7 %collective-permute-start.1 = (bf16[128,768]{1,0:T(8,128)(2,1)S(1)}, bf16[128,768]{1,0:T(8,128)(2,1)S(1)}, u32[]{:S(2)}, u32[]{:S(2)}) collective-permute-start(bf16[128,768]{1,0:T(8,128)(2,1)S(1)} %collective-permute-done), channel_id=1, source_target_pairs={{0,1},{1,2},{2,3},{3,0},{4,5},{5,6},{6,7},{7,4},{8,9},{9,10},{10,1... | collective-permute-start | bytes 589832 | tf_op jit(solution)/shard_map/ppermute | solution.py:15
  50.6 7.5 %collective-permute-start.2 = (bf16[128,768]{1,0:T(8,128)(2,1)S(1)}, bf16[128,768]{1,0:T(8,128)(2,1)S(1)}, u32[]{:S(2)}, u32[]{:S(2)}) collective-permute-start(bf16[128,768]{1,0:T(8,128)(2,1)S(1)} %collective-permute-done.1), channel_id=1, source_target_pairs={{0,1},{1,2},{2,3},{3,0},{4,5},{5,6},{6,7},{7,4},{8,9},{9,10},{10,1... | collective-permute-start | bytes 589832 | tf_op jit(solution)/shard_map/ppermute | solution.py:15
  117.4 81.4 %reduce-scatter.5.cloned.1.call-start = ((), (), s32[]{:S(2)}) async-start(), calls=%async_computation.6 | async-start | bytes 3538944 | tf_op jit(solution)/shard_map/reduce_scatter | solution.py:115
  122.5 157.0 %all-reduce.4.cloned.1.call-start = ((), (), s32[]{:S(2)}) async-start(), calls=%async_computation.7 | async-start | bytes 2752512 | tf_op jit(solution)/shard_map/psum | solution.py:145
  123.2 47.5 %copy-start.1 = (bf16[512,256]{1,0:T(8,128)(2,1)S(1)}, bf16[512,256]{1,0:T(8,128)(2,1)}, u32[]{:S(2)}) copy-start(bf16[512,256]{1,0:T(8,128)(2,1)} %param.6) | copy-start | bytes 786436
  172.0 48.7 %copy-start.2 = (bf16[512,192]{0,1:T(8,128)(2,1)S(1)}, bf16[512,192]{0,1:T(8,128)(2,1)}, u32[]{:S(2)}) copy-start(bf16[512,192]{0,1:T(8,128)(2,1)} %param.7) | copy-start | bytes 589828
Sparse Core Ops, SparseCore 0:
  28.6 26.9 all-gather.1
  117.6 32.8 reduce-scatter.2
  153.9 44.8 reduce-scatter.4
  222.0 57.4 all-reduce.3
